TPU v7x, 32 devices: a whole 2x2x4 slice. The times are simulated.
32 devices in a mesh: row: 4 (over y, x), col: 8 (over z, core).
Axes of the slice: x: 2, y: 2, z: 4, core: 2. Of those that a mesh axis runs over, the one named last changes fastest.
Arguments:
- features: bfloat16 [8192, 512], P(('row', 'col')), may hold values from -40 to 40
- w_query: bfloat16 [512, 512], replicated, may hold values from -0.25 to 0.25
- w_key: bfloat16 [512, 512], replicated, may hold values from -0.25 to 0.25
- w_value: bfloat16 [512, 512], replicated, may hold values from -0.25 to 0.25
- w_out: bfloat16 [512, 512], replicated, may hold values from -0.25 to 0.25
- pairs: int32 [4, 8, 128, 2], P('row', 'col'), may hold values from 0 to 15, as said below
- counts: int32 [4, 8], P('row', 'col'), may hold values from 16 to 128, as said below
- masks: int32 [4, 8, 128, 128, 4], P('row', 'col'), may hold values from -2147483648 to 2147483646, as said below
Outputs:
- updated: bfloat16 [8192, 512], P(('row', 'col'))
Inputs may be any that keep to these rules, and one draw needn't show every extreme that they name: Within one device's list all 128 entries are distinct pairs; the first column is a query tile below 16, the second a key tile below 8. `counts`: some device has a full list of 128 entries in every draw. `masks`: any 32-bit pattern.
All inputs are finite; a program needn't handle non-finite values.
Results may differ from a plain program's by a relative error of at most 0.012.
The roundings to bfloat16 on the way count: a program that leaves them out, or rounds other values in their place, can miss the bound.
Values may be sent and summed in bfloat16 or wider, within the bound.
No kernel may reach another device: no remote copies, remote signals or barrier semaphores. Data moves between devices by JAX's collectives and lax.ppermute only.
A program may use at most 128 MiB of HBM per device.

v0:
```python
import functools
import math

import jax
import jax.numpy as jnp
from jax import lax
from jax.experimental import pallas as pl
from jax.experimental.pallas import tpu as pltpu
from jax.sharding import PartitionSpec as P


HEADS = 8
TILE = 128
GROUP = 4
LIMIT = 24 * 1024 * 1024
VMEM = pltpu.VMEM
SMEM = pltpu.SMEM
BF16 = jnp.bfloat16
F32 = jnp.float32
LOG2E = math.log2(math.e)


def vmem():
    return pl.BlockSpec(memory_space=VMEM)


def smem():
    return pl.BlockSpec(memory_space=SMEM)


def exchange(x, axis, bits):
    size = lax.axis_size(axis)
    return lax.ppermute(x, axis, [(i, i ^ bits) for i in range(size)])


def index_kernel(where_ref, mine_ref, other_ref, out_ref, *, tiles, entries):
    row, col = where_ref[0], where_ref[1]

    def clear(i, carry):
        out_ref[i] = -1
        return carry

    lax.fori_loop(0, out_ref.shape[0], clear, 0)
    for side, ref in enumerate((mine_ref, other_ref)):

        def entry(e, carry, side=side, ref=ref):
            a, b = ref[2 * e], ref[2 * e + 1]
            chunk = (a // 2) ^ col
            tile = ((b // 2) ^ row) * 4 + side * 2 + b % 2

            @pl.when(chunk % 2 == 0)
            def _():
                out_ref[(chunk + a % 2) * tiles + tile] = e

            return carry

        lax.fori_loop(0, ref[2 * entries], entry, 0)


def index(mine, other, row, col, size, tiles, entries):
    return pl.pallas_call(
        functools.partial(index_kernel, tiles=tiles, entries=entries),
        out_shape=jax.ShapeDtypeStruct((size,), jnp.int32),
        in_specs=[smem(), smem(), smem()],
        out_specs=smem(),
        name="index",
    )(jnp.stack([row, col]).astype(jnp.int32), mine, other)


def nt_dot(a, b):
    return lax.dot_general(a, b, (((1,), (1,)), ((), ())), preferred_element_type=F32)


def project_kernel(mine_ref, other_ref, wk_ref, wvt_ref, *refs):
    k_ref, vt_ref, norm_ref = refs[-3:]
    double = k_ref.shape[3]
    width = wk_ref.shape[0]
    lane = lax.broadcasted_iota(jnp.int32, (width, TILE), 1)
    head = lax.broadcasted_iota(jnp.int32, (width, TILE), 0) // (double // 2)
    pick = jnp.where(lane == head, F32(1.01), F32(0)).astype(BF16)
    x = jnp.concatenate([mine_ref[...], other_ref[...]], axis=0)
    rows = x.shape[0]
    k = jnp.dot(x, wk_ref[...], preferred_element_type=F32).astype(BF16)
    v = nt_dot(wvt_ref[...], x).astype(BF16)
    for t in range(rows // TILE):
        for i in range(HEADS // 2):
            k_ref[t, i] = k[t * TILE : (t + 1) * TILE, i * double : (i + 1) * double]
        for h in range(HEADS):
            vt_ref[t, h] = v[h * double // 2 : (h + 1) * double // 2, t * TILE : (t + 1) * TILE]
    k = k.astype(F32)
    norms = jnp.dot((k * k).astype(BF16), pick, preferred_element_type=F32)
    norm_ref[0] = norms.reshape(rows // 8, 8, TILE).max(0)


def project(mine, other, w_key, w_value_t, so_far, at, steps):
    width = w_key.shape[0]
    size = width // HEADS
    tiles = 2 * mine.shape[0] // TILE
    return pl.pallas_call(
        project_kernel,
        grid=(1,),
        out_shape=(
            jax.ShapeDtypeStruct((steps * tiles, HEADS // 2, TILE, 2 * size), BF16),
            jax.ShapeDtypeStruct((steps * tiles, HEADS, size, TILE), BF16),
            jax.ShapeDtypeStruct((steps, 8, TILE), F32),
        ),
        in_specs=[vmem()] * 4 + [pl.BlockSpec(memory_space=pl.ANY)] * len(so_far),
        out_specs=(
            pl.BlockSpec((tiles, HEADS // 2, TILE, 2 * size), lambda i: (at, 0, 0, 0)),
            pl.BlockSpec((tiles, HEADS, size, TILE), lambda i: (at, 0, 0, 0)),
            pl.BlockSpec((1, 8, TILE), lambda i: (at, 0, 0)),
        ),
        input_output_aliases={4 + i: i for i in range(len(so_far))},
        compiler_params=pltpu.CompilerParams(vmem_limit_bytes=LIMIT),
        name="project",
    )(mine, other, w_key, w_value_t, *so_far)


def split3(x):
    hi = x.astype(BF16)
    rest = x - hi.astype(F32)
    mid = rest.astype(BF16)
    low = (rest - mid.astype(F32)).astype(BF16)
    return [hi, mid, low]


def attend_kernel(
    index_ref, mine_ref, other_ref, f_ref, wqt_ref, k_ref, vt_ref, norm_ref, out_ref, q_ref, mask_ref,
    acc_ref, max_ref, list_ref, *, chunk, sinks
):
    tiles, _, _, double = k_ref.shape
    size = double // 2
    width = HEADS * size
    nodes = f_ref.shape[0]
    factor = LOG2E / math.sqrt(size)

    start = chunk * (nodes // TILE) * tiles

    def gather(n, found):
        list_ref[found] = n
        used = index_ref[start + n] >= 0
        for t in range(1, nodes // TILE):
            used = used | (index_ref[start + t * tiles + n] >= 0)
        return found + jnp.where(used, 1, 0)

    found = lax.fori_loop(0, tiles, gather, 0)
    groups = (found + GROUP - 1) // GROUP
    bit = lax.shift_left(jnp.int32(1), lax.broadcasted_iota(jnp.int32, (32, TILE), 0))

    def mask(i, carry):
        live = i < found
        n = jnp.where(live, list_ref[i], 0)
        list_ref[i] = n
        for t in range(nodes // TILE):
            e = index_ref[start + t * tiles + n]
            at = jnp.maximum(e, 0)
            words = jnp.where(n // 2 % 2 == 0, mine_ref[at], other_ref[at])
            words = jnp.where(live & (e >= 0), words, 0)
            for w in range(4):
                row = jnp.broadcast_to(words[w : w + 1, :], (32, TILE))
                mask_ref[i, w * 32 : (w + 1) * 32, t * TILE : (t + 1) * TILE] = jnp.where(
                    (row & bit) != 0, F32(1), F32(0)
                ).astype(BF16)
        return carry

    lax.fori_loop(0, groups * GROUP, mask, 0)

    q = nt_dot(wqt_ref[...], f_ref[...]).astype(BF16)
    lower = lax.broadcasted_iota(jnp.int32, (double, nodes), 0) < size
    first = lax.broadcasted_iota(jnp.int32, (size + 16, nodes), 0) == size
    longest = norm_ref[...].max(0).max(0, keepdims=True).max(1, keepdims=True)
    bounds = []
    for h in range(HEADS):
        pair = q[(h // 2) * double : (h // 2 + 1) * double, :]
        q_ref[h // 2, 0:double, h % 2 * nodes : (h % 2 + 1) * nodes] = jnp.where(lower == (h % 2 == 0), pair, jnp.zeros_like(pair))
        mine = q[h * size : (h + 1) * size, :].astype(F32)
        bounds.append(jnp.sqrt((mine * mine).sum(0, keepdims=True) * longest) * F32(1.02))
    bound = jnp.concatenate(bounds, axis=0)
    calm = jnp.max(bound) * F32(factor) <= F32(80)

    @pl.when(calm)
    def _():
        sink = jnp.exp2(bound * -factor) * F32(sinks)
        pieces = [jnp.zeros_like(x) - x for x in split3(bound)]
        for h in range(HEADS):
            column = jnp.concatenate(
                [x[h : h + 1, :].astype(F32) for x in pieces] + [jnp.zeros((13, nodes), F32)], axis=0
            )
            q_ref[h // 2, double : double + 16, h % 2 * nodes : (h % 2 + 1) * nodes] = column.astype(BF16)
            q_ref[h // 2, double + 16 : 2 * double, h % 2 * nodes : (h % 2 + 1) * nodes] = jnp.zeros((double - 16, nodes), BF16)
            max_ref[h] = bound[h : h + 1, :] * F32(factor)
            acc_ref[h] = jnp.where(first, sink[h : h + 1, :], F32(0))
        ones = jnp.ones((16, TILE * GROUP), BF16)
        lane = lax.broadcasted_iota(jnp.int32, (TILE, double), 1)
        units = jnp.where(lane < 3, F32(1), F32(0)).astype(BF16)

        def step(i, carry):
            picked = [list_ref[i * GROUP + g] for g in range(GROUP)]
            keep = jnp.concatenate([mask_ref[i * GROUP + g] for g in range(GROUP)], axis=0)
            keep = jnp.concatenate([keep, keep], axis=1)

            def scores(m):
                keys = [jnp.concatenate([k_ref[n, m], units], axis=1) for n in picked]
                return jnp.dot(jnp.concatenate(keys, axis=0), q_ref[m], preferred_element_type=F32)

            ahead = scores(0)
            for m in range(HEADS // 2):
                s = ahead
                if m + 1 < HEADS // 2:
                    ahead = scores(m + 1)
                p = jnp.exp2(s * F32(factor)).astype(BF16) * keep
                for o in range(2):
                    h = 2 * m + o
                    values = jnp.concatenate([vt_ref[n, h] for n in picked], axis=1)
                    values = jnp.concatenate([values, ones], axis=0)
                    acc_ref[h] = acc_ref[h] + jnp.dot(
                        values, p[:, o * nodes : (o + 1) * nodes], preferred_element_type=F32
                    )
            return carry

        lax.fori_loop(0, groups, step, 0)

    @pl.when(jnp.logical_not(calm))
    def _():
        for h in range(HEADS):
            max_ref[h] = jnp.zeros((1, nodes), F32)
            acc_ref[h] = jnp.where(first, F32(sinks), F32(0))
        ones = jnp.ones((16, TILE), BF16)

        def step(i, carry):
            n = list_ref[i]

            def pair(m, carry):
                both = jnp.dot(k_ref[n, m], q_ref[m, 0:double, :], preferred_element_type=F32)
                for o in range(2):
                    h = 2 * m + o
                    s = both[:, o * nodes : (o + 1) * nodes] * F32(factor)
                    s = jnp.where(mask_ref[i].astype(F32) > 0, s, F32(-jnp.inf))
                    old = max_ref[h]
                    top = jnp.maximum(old, s.max(0, keepdims=True))
                    max_ref[h] = top
                    p = jnp.exp2(s - top).astype(BF16)
                    values = jnp.concatenate([vt_ref[n, h], ones], axis=0)
                    acc_ref[h] = acc_ref[h] * jnp.exp2(old - top) + jnp.dot(
                        values, p, preferred_element_type=F32
                    )
                return carry

            return lax.fori_loop(0, HEADS // 2, pair, carry)

        lax.fori_loop(0, found, step, 0)

    tops, dens = [], []
    for h in range(HEADS):
        den = acc_ref[h, size : size + 1, :]
        out_ref[h * size : (h + 1) * size, :] = (acc_ref[h, 0:size, :] / den).astype(BF16)
        tops.append(max_ref[h])
        dens.append(den)
    stats = split3(jnp.concatenate(tops + dens, axis=0))
    for i, part in enumerate(stats):
        out_ref[width + i * 16 : width + (i + 1) * 16, :] = part


def attend(table, mine, other, feats, w_query_t, keys, values_t, norms, chunk, sinks):
    nodes, width = feats.shape
    size = width // HEADS
    room = (keys.shape[0] + GROUP - 1) // GROUP * GROUP
    return pl.pallas_call(
        functools.partial(attend_kernel, chunk=chunk, sinks=sinks),
        out_shape=jax.ShapeDtypeStruct((width + 48, nodes), BF16),
        in_specs=[smem()] + [vmem()] * 7,
        out_specs=vmem(),
        scratch_shapes=[
            VMEM((HEADS // 2, 4 * size, 2 * nodes), BF16),
            VMEM((room, TILE, nodes), BF16),
            VMEM((HEADS, size + 16, nodes), F32),
            VMEM((HEADS, 1, nodes), F32),
            SMEM((room + 1,), jnp.int32),
        ],
        compiler_params=pltpu.CompilerParams(vmem_limit_bytes=LIMIT),
        name="attend",
    )(table, mine, other, feats, w_query_t, keys, values_t, norms)


def finish_kernel(*refs):
    parts, (w_ref, out_ref) = refs[:-2], refs[-2:]
    width = w_ref.shape[0]
    size = width // HEADS
    tops, dens = [], []
    for part in parts:
        stats = (
            part[width : width + 16, :].astype(F32)
            + part[width + 16 : width + 32, :].astype(F32)
            + part[width + 32 : width + 48, :].astype(F32)
        )
        tops.append(stats[0:HEADS])
        dens.append(stats[HEADS : 2 * HEADS])
    top = functools.reduce(jnp.maximum, tops)
    weights = [jnp.exp2(t - top) * d for t, d in zip(tops, dens)]
    total = functools.reduce(jnp.add, weights)
    rows = []
    for h in range(HEADS):
        num = functools.reduce(
            jnp.add,
            [
                part[h * size : (h + 1) * size, :].astype(F32) * weight[h : h + 1, :]
                for part, weight in zip(parts, weights)
            ],
        )
        rows.append((num / total[h : h + 1, :]).astype(BF16))
    attended = jnp.concatenate(rows, axis=0)
    out_ref[...] = lax.dot_general(
        attended, w_ref[...], (((0,), (0,)), ((), ())), preferred_element_type=F32
    ).astype(BF16)


def finish(parts, w_out):
    nodes = parts[0].shape[1]
    return pl.pallas_call(
        finish_kernel,
        out_shape=jax.ShapeDtypeStruct((nodes, w_out.shape[1]), BF16),
        in_specs=[vmem()] * (len(parts) + 1),
        out_specs=vmem(),
        name="finish",
    )(*parts, w_out)


def body(features, w_query, w_key, w_value, w_out, pairs, counts, masks):
    nrow, ncol = lax.axis_size("row"), lax.axis_size("col")
    nodes, _ = features.shape
    per = nodes // TILE
    row, col = lax.axis_index("row"), lax.axis_index("col")
    chips = ncol // 2
    tiles = 2 * nrow * per
    entries = pairs.shape[2]

    asking = [features] + [None] * (chips - 1)
    near = [features] + [None] * (nrow - 1)
    far = list(range(chips // 2, chips)) + list(range(1, chips // 2))
    for s in range(1, nrow):
        near[s] = exchange(features, "row", s)
    for s in far:
        asking[s] = exchange(features, "col", 2 * s)
    mine = jnp.swapaxes(masks[0, 0], 1, 2)
    other = exchange(mine, "col", 1)
    listed = jnp.concatenate([pairs.reshape(-1), counts.reshape(-1)])
    theirs = exchange(listed, "col", 1)
    table = index(listed, theirs, row, col, chips * per * tiles, tiles, entries)

    w_value_t, w_query_t = w_value.T, w_query.T
    ready = ()
    for s in range(nrow):
        twin = exchange(near[s], "col", 1)
        ready = project(near[s], twin, w_key, w_value_t, ready, s, nrow)

    parts = [None] * chips
    for s in far + [0]:
        part = attend(table, mine, other, asking[s], w_query_t, *ready, s, 2)
        parts[s] = part if s == 0 else exchange(part, "col", 2 * s)
    return finish(parts, w_out)


def solution(mesh):
    in_specs = (
        P(("row", "col"), None),
        P(),
        P(),
        P(),
        P(),
        P("row", "col", None, None),
        P("row", "col"),
        P("row", "col", None, None, None),
    )
    out_specs = P(("row", "col"), None)

    return jax.shard_map(body, mesh=mesh, in_specs=in_specs, out_specs=out_specs, check_vma=False)
```

profile of v0, /device:TPU:7, one launch (start us, length us, event | category | flops | bytes accessed | tf_op | source)
XLA Modules:
  0.0 135.3 jit_solution(17958006836492678353)
XLA Ops:
  0.0 0.3 collective-permute-start.6
  0.3 0.0 collective-permute-start.4
  0.3 2.3 %collective-permute-start.2 = (bf16[256,512]{1,0:T(8,128)(2,1)}, bf16[256,512]{1,0:T(8,128)(2,1)S(1)}, u32[]{:S(2)}, u32[]{:S(2)}) collective-permute-start(bf16[256,512]{1,0:T(8,128)(2,1)} %f_ref.1), channel_id=1, source_target_pairs={{0,24},{8,16},{16,8},{24,0},{1,25},{9,17},{17,9},{25,1},{2,26},{10... | collective-permute-start | bytes 786440 | tf_op jit(solution)/shard_map/ppermute | solution.py:33
  2.7 1.5 %collective-permute-start.8 = (bf16[256,512]{1,0:T(8,128)(2,1)}, bf16[256,512]{1,0:T(8,128)(2,1)S(1)}, u32[]{:S(2)}, u32[]{:S(2)}) collective-permute-start(bf16[256,512]{1,0:T(8,128)(2,1)} %f_ref.1), channel_id=1, source_target_pairs={{0,1},{1,0},{2,3},{3,2},{4,5},{5,4},{6,7},{7,6},{8,9},{9,8},{10,11... | collective-permute-start | bytes 786440 | tf_op jit(solution)/shard_map/ppermute | solution.py:33
  4.2 3.2 %collective-permute-done.6.mine_ref = bf16[256,512]{1,0:T(8,128)(2,1)S(1)} collective-permute-done((bf16[256,512]{1,0:T(8,128)(2,1)}, bf16[256,512]{1,0:T(8,128)(2,1)S(1)}, u32[]{:S(2)}, u32[]{:S(2)}) %collective-permute-start.6) | collective-permute-done | bytes 262176 | tf_op jit(solution)/shard_map/ppermute | solution.py:33
  7.4 2.7 %collective-permute-start.7 = (bf16[256,512]{1,0:T(8,128)(2,1)S(1)}, bf16[256,512]{1,0:T(8,128)(2,1)S(1)}, u32[]{:S(2)}, u32[]{:S(2)}) collective-permute-start(bf16[256,512]{1,0:T(8,128)(2,1)S(1)} %collective-permute-done.6.mine_ref), channel_id=1, source_target_pairs={{0,1},{1,0},{2,3},{3,2},{4,5},{5,4},{6,7},{7,6},{8,9},{9,8},{10,11... | collective-permute-start | bytes 786440 | tf_op jit(solution)/shard_map/ppermute | solution.py:33
  10.1 0.0 collective-permute-done.4.mine_ref
  10.1 4.7 %collective-permute-start.5 = (bf16[256,512]{1,0:T(8,128)(2,1)S(1)}, bf16[256,512]{1,0:T(8,128)(2,1)S(1)}, u32[]{:S(2)}, u32[]{:S(2)}) collective-permute-start(bf16[256,512]{1,0:T(8,128)(2,1)S(1)} %collective-permute-done.4.mine_ref), channel_id=1, source_target_pairs={{0,1},{1,0},{2,3},{3,2},{4,5},{5,4},{6,7},{7,6},{8,9},{9,8},{10,11... | collective-permute-start | bytes 786440 | tf_op jit(solution)/shard_map/ppermute | solution.py:33
  14.8 0.8 copy.20
  15.6 0.1 reshape.6
  16.4 0.1 collective-permute-start
  16.5 0.0 collective-permute-done.2.mine_ref
  16.5 0.5 collective-permute-start.3
  17.0 0.6 collective-permute-done.other_ref
  17.6 0.2 collective-permute-start.1
  17.8 0.0 collective-permute-done.8.other_ref
  17.8 3.3 %collective-permute-start.13 = (bf16[256,512]{1,0:T(8,128)(2,1)}, bf16[256,512]{1,0:T(8,128)(2,1)}, u32[]{:S(2)}, u32[]{:S(2)}) collective-permute-start(bf16[256,512]{1,0:T(8,128)(2,1)} %f_ref.1), channel_id=1, source_target_pairs={{0,6},{1,7},{2,4},{3,5},{4,2},{5,3},{6,0},{7,1},{8,14},{9,15},{10,... | collective-permute-start | bytes 786440 | tf_op jit(solution)/shard_map/ppermute | solution.py:33
  21.1 0.0 collective-permute-done.7.other_ref
  21.1 0.0 collective-permute-start.11
  21.2 0.4 collective-permute-start.9
  21.5 1.3 copy.22
  22.8 1.3 copy.21
  24.1 0.6 pad_add_fusion.1.where_ref
  24.7 5.9 %index.1.index_ref = s32[128]{0:T(128)} custom-call(s32[2]{0:T(128)} %pad_add_fusion.1.where_ref, s32[257]{0:T(512)} %copy-done.11, s32[257]{0:T(512)} %copy-done.12), custom_call_target="tpu_custom_call" | custom-call | tf_op jit(solution)/shard_map/index/pallas_call | solution.py:61
  30.6 0.9 copy-done.7
  31.6 0.8 project.4
  32.4 0.0 copy-start.5
  32.5 0.9 copy-done.5
  33.4 0.8 project.5
  34.2 0.9 project.6
  35.1 0.0 collective-permute-done.3.other_ref
  35.1 0.0 copy-start.1
  35.1 1.8 %project.7 = (bf16[16,4,128,128]{3,2,1,0:T(8,128)(2,1)S(1)}, bf16[16,8,64,128]{3,2,1,0:T(8,128)(2,1)S(1)}, f32[4,8,128]{2,1,0:T(8,128)S(1)}) custom-call(bf16[256,512]{1,0:T(8,128)(2,1)S(1)} %collective-permute-done.2.mine_ref, bf16[256,512]{1,0:T(8,128)(2,1)} %collective-permute-done.3.other_ref, ...), custom_call_target="tpu_custom_call", output_to_operand_aliasing={{0}: (4, {}), {1}: (5, {}), {2}: (6, {})} | custom-call | tf_op jit(solution)/shard_map/project/pallas_call | solution.py:99
  37.0 0.0 collective-permute-done.1.other_ref
  37.0 0.0 collective-permute-done.13.f_ref
  37.0 24.8 %attend.7 = bf16[560,256]{1,0:T(8,128)(2,1)S(1)} custom-call(s32[128]{0:T(128)S(1)} %copy-done.8, s32[128,4,128]{2,1,0:T(4,128)S(1)} %bitcast.20, s32[128,4,128]{2,1,0:T(4,128)S(1)} %collective-permute-done.1.other_ref, bf16[256,512]{1,0:T(8,128)(2,1)} %collective-permute-done.13.f_ref, bf16[512,512]{1,0:T(8,128)(2,1)S(1)} %bitcast.11, ...), custom_call_target="tpu_custom_call" | custom-call | tf_op jit(solution)/shard_map/attend/pallas_call | solution.py:268
  61.8 0.1 collective-permute-start.14
  61.9 0.0 collective-permute-done.11.f_ref
  61.9 23.3 %attend.6 = bf16[560,256]{1,0:T(8,128)(2,1)S(1)} custom-call(s32[128]{0:T(128)S(1)} %copy-done.8, s32[128,4,128]{2,1,0:T(4,128)S(1)} %bitcast.21, s32[128,4,128]{2,1,0:T(4,128)S(1)} %collective-permute-done.1.other_ref, bf16[256,512]{1,0:T(8,128)(2,1)} %collective-permute-done.11.f_ref, bf16[512,512]{1,0:T(8,128)(2,1)S(1)} %bitcast.12, ...), custom_call_target="tpu_custom_call" | custom-call | tf_op jit(solution)/shard_map/attend/pallas_call | solution.py:268
  85.2 0.1 collective-permute-start.12
  85.3 24.4 %attend.5 = bf16[560,256]{1,0:T(8,128)(2,1)S(1)} custom-call(s32[128]{0:T(128)S(1)} %copy-done.8, s32[128,4,128]{2,1,0:T(4,128)S(1)} %bitcast.22, s32[128,4,128]{2,1,0:T(4,128)S(1)} %collective-permute-done.1.other_ref, bf16[256,512]{1,0:T(8,128)(2,1)S(1)} %collective-permute-done.9.f_ref, bf16[512,512]{1,0:T(8,128)(2,1)S(1)} %bitcast.13, ...), custom_call_target="tpu_custom_call" | custom-call | tf_op jit(solution)/shard_map/attend/pallas_call | solution.py:268
  109.7 0.1 collective-permute-start.10
  109.8 21.4 %attend.4.refs_0_ = bf16[560,256]{1,0:T(8,128)(2,1)S(1)} custom-call(s32[128]{0:T(128)S(1)} %copy-done.8, s32[128,4,128]{2,1,0:T(4,128)S(1)} %bitcast.23, s32[128,4,128]{2,1,0:T(4,128)S(1)} %collective-permute-done.1.other_ref, bf16[256,512]{1,0:T(8,128)(2,1)S(1)} %copy-done.3, bf16[512,512]{1,0:T(8,128)(2,1)S(1)} %bitcast.14, ...), custom_call_target="tpu_custom_call" | custom-call | tf_op jit(solution)/shard_map/attend/pallas_call | solution.py:268
  131.2 0.7 copy-done.2
  131.9 0.0 collective-permute-done.10.refs_1_
  131.9 0.7 copy-done.9
  132.6 0.1 copy-done.10
  132.7 2.6 %finish.1 = bf16[256,512]{1,0:T(8,128)(2,1)} custom-call(bf16[560,256]{1,0:T(8,128)(2,1)} %copy-done.2, bf16[560,256]{1,0:T(8,128)(2,1)} %collective-permute-done.10.refs_1_, bf16[560,256]{1,0:T(8,128)(2,1)} %copy-done.10, bf16[560,256]{1,0:T(8,128)(2,1)} %copy-done.9, bf16[512,512]{1,0:T(8,128)(2,1)} %refs_4_.1), custom_call_target="tpu_custom_call" | custom-call | tf_op jit(solution)/shard_map/finish/pallas_call | solution.py:319
  (24 shorter events, 0.1 us)
Async XLA Ops:
  0.0 30.6 %copy-start.3 = (bf16[256,512]{1,0:T(8,128)(2,1)S(1)}, bf16[256,512]{1,0:T(8,128)(2,1)}, u32[]{:S(2)}) copy-start(bf16[256,512]{1,0:T(8,128)(2,1)} %f_ref.1) | copy-start | bytes 786436
  0.0 30.6 %copy-start = (bf16[512,512]{1,0:T(8,128)(2,1)S(1)}, bf16[512,512]{1,0:T(8,128)(2,1)}, u32[]{:S(2)}) copy-start(bf16[512,512]{1,0:T(8,128)(2,1)} %wk_ref.7) | copy-start | bytes 1572868
  0.0 7.4 %collective-permute-start.6 = (bf16[256,512]{1,0:T(8,128)(2,1)}, bf16[256,512]{1,0:T(8,128)(2,1)S(1)}, u32[]{:S(2)}, u32[]{:S(2)}) collective-permute-start(bf16[256,512]{1,0:T(8,128)(2,1)} %f_ref.1), channel_id=1, source_target_pairs={{0,8},{8,0},{16,24},{24,16},{1,9},{9,1},{17,25},{25,17},{2,10},{10... | collective-permute-start | bytes 786440 | tf_op jit(solution)/shard_map/ppermute | solution.py:33
  0.3 9.8 %collective-permute-start.4 = (bf16[256,512]{1,0:T(8,128)(2,1)}, bf16[256,512]{1,0:T(8,128)(2,1)S(1)}, u32[]{:S(2)}, u32[]{:S(2)}) collective-permute-start(bf16[256,512]{1,0:T(8,128)(2,1)} %f_ref.1), channel_id=1, source_target_pairs={{0,16},{8,24},{16,0},{24,8},{1,17},{9,25},{17,1},{25,9},{2,18},{10... | collective-permute-start | bytes 786440 | tf_op jit(solution)/shard_map/ppermute | solution.py:33
  0.3 16.2 %collective-permute-start.2 = (bf16[256,512]{1,0:T(8,128)(2,1)}, bf16[256,512]{1,0:T(8,128)(2,1)S(1)}, u32[]{:S(2)}, u32[]{:S(2)}) collective-permute-start(bf16[256,512]{1,0:T(8,128)(2,1)} %f_ref.1), channel_id=1, source_target_pairs={{0,24},{8,16},{16,8},{24,0},{1,25},{9,17},{17,9},{25,1},{2,26},{10... | collective-permute-start | bytes 786440 | tf_op jit(solution)/shard_map/ppermute | solution.py:33
  2.7 15.2 %collective-permute-start.8 = (bf16[256,512]{1,0:T(8,128)(2,1)}, bf16[256,512]{1,0:T(8,128)(2,1)S(1)}, u32[]{:S(2)}, u32[]{:S(2)}) collective-permute-start(bf16[256,512]{1,0:T(8,128)(2,1)} %f_ref.1), channel_id=1, source_target_pairs={{0,1},{1,0},{2,3},{3,2},{4,5},{5,4},{6,7},{7,6},{8,9},{9,8},{10,11... | collective-permute-start | bytes 786440 | tf_op jit(solution)/shard_map/ppermute | solution.py:33
  7.4 13.7 %collective-permute-start.7 = (bf16[256,512]{1,0:T(8,128)(2,1)S(1)}, bf16[256,512]{1,0:T(8,128)(2,1)S(1)}, u32[]{:S(2)}, u32[]{:S(2)}) collective-permute-start(bf16[256,512]{1,0:T(8,128)(2,1)S(1)} %collective-permute-done.6.mine_ref), channel_id=1, source_target_pairs={{0,1},{1,0},{2,3},{3,2},{4,5},{5,4},{6,7},{7,6},{8,9},{9,8},{10,11... | collective-permute-start | bytes 786440 | tf_op jit(solution)/shard_map/ppermute | solution.py:33
  10.1 11.1 %collective-permute-start.5 = (bf16[256,512]{1,0:T(8,128)(2,1)S(1)}, bf16[256,512]{1,0:T(8,128)(2,1)S(1)}, u32[]{:S(2)}, u32[]{:S(2)}) collective-permute-start(bf16[256,512]{1,0:T(8,128)(2,1)S(1)} %collective-permute-done.4.mine_ref), channel_id=1, source_target_pairs={{0,1},{1,0},{2,3},{3,2},{4,5},{5,4},{6,7},{7,6},{8,9},{9,8},{10,11... | collective-permute-start | bytes 786440 | tf_op jit(solution)/shard_map/ppermute | solution.py:33
  16.4 8.3 %copy-start.11 = (s32[257]{0:T(512)}, s32[257]{0:T(512)S(1)}, u32[]{:S(2)}) copy-start(s32[257]{0:T(512)S(1)} %pad_add_fusion.mine_ref) | copy-start | bytes 3088
  16.4 1.2 collective-permute-start
  16.5 18.6 %collective-permute-start.3 = (bf16[256,512]{1,0:T(8,128)(2,1)S(1)}, bf16[256,512]{1,0:T(8,128)(2,1)}, u32[]{:S(2)}, u32[]{:S(2)}) collective-permute-start(bf16[256,512]{1,0:T(8,128)(2,1)S(1)} %collective-permute-done.2.mine_ref), channel_id=1, source_target_pairs={{0,1},{1,0},{2,3},{3,2},{4,5},{5,4},{6,7},{7,6},{8,9},{9,8},{10,11... | collective-permute-start | bytes 786440 | tf_op jit(solution)/shard_map/ppermute | solution.py:33
  17.6 7.0 %copy-start.12 = (s32[257]{0:T(512)}, s32[257]{0:T(512)S(1)}, u32[]{:S(2)}) copy-start(s32[257]{0:T(512)S(1)} %collective-permute-done.other_ref) | copy-start | bytes 3088
  17.6 19.3 %collective-permute-start.1 = (s32[128,4,128]{2,1,0:T(4,128)}, s32[128,4,128]{2,1,0:T(4,128)S(1)}, u32[]{:S(2)}, u32[]{:S(2)}) collective-permute-start(s32[128,4,128]{2,1,0:T(4,128)} %bitcast.19), channel_id=1, source_target_pairs={{0,1},{1,0},{2,3},{3,2},{4,5},{5,4},{6,7},{7,6},{8,9},{9,8},{10,11... | collective-permute-start | bytes 786440 | tf_op jit(solution)/shard_map/ppermute | solution.py:33
  17.8 5.0 %copy-start.6 = (bf16[256,512]{1,0:T(8,128)(2,1)}, bf16[256,512]{1,0:T(8,128)(2,1)S(1)}, u32[]{:S(2)}) copy-start(bf16[256,512]{1,0:T(8,128)(2,1)S(1)} %collective-permute-done.8.other_ref) | copy-start | bytes 786436
  17.8 19.2 %collective-permute-start.13 = (bf16[256,512]{1,0:T(8,128)(2,1)}, bf16[256,512]{1,0:T(8,128)(2,1)}, u32[]{:S(2)}, u32[]{:S(2)}) collective-permute-start(bf16[256,512]{1,0:T(8,128)(2,1)} %f_ref.1), channel_id=1, source_target_pairs={{0,6},{1,7},{2,4},{3,5},{4,2},{5,3},{6,0},{7,1},{8,14},{9,15},{10,... | collective-permute-start | bytes 786440 | tf_op jit(solution)/shard_map/ppermute | solution.py:33
  21.1 1.7 %copy-start.4 = (bf16[256,512]{1,0:T(8,128)(2,1)}, bf16[256,512]{1,0:T(8,128)(2,1)S(1)}, u32[]{:S(2)}) copy-start(bf16[256,512]{1,0:T(8,128)(2,1)S(1)} %collective-permute-done.7.other_ref) | copy-start | bytes 786436
  21.1 40.8 %collective-permute-start.11 = (bf16[256,512]{1,0:T(8,128)(2,1)}, bf16[256,512]{1,0:T(8,128)(2,1)}, u32[]{:S(2)}, u32[]{:S(2)}) collective-permute-start(bf16[256,512]{1,0:T(8,128)(2,1)} %f_ref.1), channel_id=1, source_target_pairs={{0,4},{1,5},{2,6},{3,7},{4,0},{5,1},{6,2},{7,3},{8,12},{9,13},{10,... | collective-permute-start | bytes 786440 | tf_op jit(solution)/shard_map/ppermute | solution.py:33
  21.2 64.2 %collective-permute-start.9 = (bf16[256,512]{1,0:T(8,128)(2,1)}, bf16[256,512]{1,0:T(8,128)(2,1)S(1)}, u32[]{:S(2)}, u32[]{:S(2)}) collective-permute-start(bf16[256,512]{1,0:T(8,128)(2,1)} %f_ref.1), channel_id=1, source_target_pairs={{0,2},{1,3},{2,0},{3,1},{4,6},{5,7},{6,4},{7,5},{8,10},{9,11},{10,... | collective-permute-start | bytes 786440 | tf_op jit(solution)/shard_map/ppermute | solution.py:33
  30.6 1.0 copy-start.7
  32.4 1.0 copy-start.5
  35.1 1.9 %copy-start.1 = (s32[1,1,128,128,4]{3,4,2,1,0:T(4,128)S(1)}, s32[1,1,128,128,4]{3,4,2,1,0:T(4,128)}, u32[]{:S(2)}) copy-start(s32[1,1,128,128,4]{3,4,2,1,0:T(4,128)} %param.15) | copy-start | bytes 786436
  35.1 1.9 %copy-start.8 = (s32[128]{0:T(128)S(1)}, s32[128]{0:T(128)}, u32[]{:S(2)}) copy-start(s32[128]{0:T(128)} %index.1.index_ref) | copy-start | bytes 1540
  61.8 70.1 %collective-permute-start.14 = (bf16[560,256]{1,0:T(8,128)(2,1)S(1)}, bf16[560,256]{1,0:T(8,128)(2,1)S(1)}, u32[]{:S(2)}, u32[]{:S(2)}) collective-permute-start(bf16[560,256]{1,0:T(8,128)(2,1)S(1)} %attend.7), channel_id=1, source_target_pairs={{0,6},{1,7},{2,4},{3,5},{4,2},{5,3},{6,0},{7,1},{8,14},{9,15},{10,... | collective-permute-start | bytes 860168 | tf_op jit(solution)/shard_map/ppermute | solution.py:33
  85.2 46.7 %collective-permute-start.12 = (bf16[560,256]{1,0:T(8,128)(2,1)S(1)}, bf16[560,256]{1,0:T(8,128)(2,1)S(1)}, u32[]{:S(2)}, u32[]{:S(2)}) collective-permute-start(bf16[560,256]{1,0:T(8,128)(2,1)S(1)} %attend.6), channel_id=1, source_target_pairs={{0,4},{1,5},{2,6},{3,7},{4,0},{5,1},{6,2},{7,3},{8,12},{9,13},{10,... | collective-permute-start | bytes 860168 | tf_op jit(solution)/shard_map/ppermute | solution.py:33
  109.7 22.2 %collective-permute-start.10 = (bf16[560,256]{1,0:T(8,128)(2,1)S(1)}, bf16[560,256]{1,0:T(8,128)(2,1)}, u32[]{:S(2)}, u32[]{:S(2)}) collective-permute-start(bf16[560,256]{1,0:T(8,128)(2,1)S(1)} %attend.5), channel_id=1, source_target_pairs={{0,2},{1,3},{2,0},{3,1},{4,6},{5,7},{6,4},{7,5},{8,10},{9,11},{10,... | collective-permute-start | bytes 860168 | tf_op jit(solution)/shard_map/ppermute | solution.py:33
  131.2 0.7 copy-start.2
  131.9 0.7 copy-start.9
  131.9 0.8 copy-start.10
where the time goes:
time: 136 us; the launch traced here: 135 us
  Pallas kernels  107 us (79%)
  starting transfers between devices  16.2 us (12%)
  local copies, waits for them, and re-layouts  6.82 us (5%)
  waiting for transfers between devices  3.92 us (3%)
    pallas_call x4, Pallas kernels, attend(): pl.pallas_call(functools.partial(attend_kernel, chunk=chunk, sinks=sinks)...  93.9 us
    ppermute x15, starting transfers between devices, exchange(): return lax.ppermute(x, axis, [(i, i ^ bits) for i in range(size)])  16.2 us
    unnamed x29, local copies, waits for them, and re-layouts  6.69 us
    pallas_call x1, Pallas kernels, index(): pl.pallas_call(functools.partial(index_kernel, tiles=tiles, entries=entri...  5.93 us
    pallas_call x4, Pallas kernels, project(): pl.pallas_call(project_kernel, grid=(1,), out_shape=(jax.ShapeDtypeStruct...  4.39 us
    ppermute x15, waiting for transfers between devices, exchange(): return lax.ppermute(x, axis, [(i, i ^ bits) for i in range(size)])  3.92 us
  transfers between devices with their start and end apart: 15, of which 2 were waited for; matrix products, arithmetic and copies ran while one was open for 3% of the time, Pallas kernels for 77%

commit v1 on v0

--- a/solution.py
+++ b/solution.py
@@ -33,38 +33,59 @@
     return lax.ppermute(x, axis, [(i, i ^ bits) for i in range(size)])
 
 
-def index_kernel(where_ref, mine_ref, other_ref, out_ref, *, tiles, entries):
-    row, col = where_ref[0], where_ref[1]
-
-    def clear(i, carry):
-        out_ref[i] = -1
-        return carry
-
-    lax.fori_loop(0, out_ref.shape[0], clear, 0)
-    for side, ref in enumerate((mine_ref, other_ref)):
-
-        def entry(e, carry, side=side, ref=ref):
-            a, b = ref[2 * e], ref[2 * e + 1]
-            chunk = (a // 2) ^ col
-            tile = ((b // 2) ^ row) * 4 + side * 2 + b % 2
-
-            @pl.when(chunk % 2 == 0)
-            def _():
-                out_ref[(chunk + a % 2) * tiles + tile] = e
-
-            return carry
-
-        lax.fori_loop(0, ref[2 * entries], entry, 0)
-
-
-def index(mine, other, row, col, size, tiles, entries):
+def index_kernel(mine_ref, count_ref, other_ref, other_count_ref, out_ref, *, tiles):
+    row, col = lax.axis_index("row"), lax.axis_index("col")
+    entries = mine_ref.shape[1]
+    order = lax.broadcasted_iota(jnp.int32, (1, entries), 1)
+    number = lax.broadcasted_iota(jnp.int32, (entries, TILE), 0) + 1
+    lane = lax.broadcasted_iota(jnp.int32, (entries, TILE), 1)
+    spots = []
+    for side, (ref, count) in enumerate(((mine_ref, count_ref), (other_ref, other_count_ref))):
+        a, b = ref[0:1, :], ref[1:2, :]
+        chunk = (a >> 1) ^ col
+        tile = (((b >> 1) ^ row) << 2) + side * 2 + (b & 1)
+        good = (order < count[0, 0]) & ((chunk & 1) == 0)
+        spot = jnp.where(good, (chunk + (a & 1)) * tiles + tile, -1)
+        spots.append(jnp.broadcast_to(spot.astype(F32), (TILE, entries)).T.astype(jnp.int32))
+    for block in range(out_ref.shape[1] // TILE):
+        found = jnp.zeros((1, TILE), jnp.int32)
+        for spot in spots:
+            here = jnp.where(spot == lane + block * TILE, number, 0)
+            found = found + here.sum(0, keepdims=True)
+        out_ref[0:1, block * TILE : (block + 1) * TILE] = found - 1
+
+
+def cost(microseconds):
+    return pl.CostEstimate(flops=int(microseconds * 9e8), bytes_accessed=0, transcendentals=0)
+
+
+def index(mine, count, other, other_count, size, tiles):
     return pl.pallas_call(
-        functools.partial(index_kernel, tiles=tiles, entries=entries),
-        out_shape=jax.ShapeDtypeStruct((size,), jnp.int32),
-        in_specs=[smem(), smem(), smem()],
-        out_specs=smem(),
+        functools.partial(index_kernel, tiles=tiles),
+        out_shape=jax.ShapeDtypeStruct((1, (size + TILE - 1) // TILE * TILE), jnp.int32),
+        in_specs=[vmem(), smem(), vmem(), smem()],
+        out_specs=vmem(),
+        cost_estimate=cost(3),
+        compiler_params=pltpu.CompilerParams(vmem_limit_bytes=LIMIT),
         name="index",
-    )(jnp.stack([row, col]).astype(jnp.int32), mine, other)
+    )(mine, count, other, other_count)
+
+
+def turn_kernel(after_ref, a_ref, b_ref, at_ref, bt_ref):
+    at_ref[...] = a_ref[...].T
+    bt_ref[...] = b_ref[...].T
+
+
+def turn(after, a, b):
+    return pl.pallas_call(
+        turn_kernel,
+        out_shape=tuple(jax.ShapeDtypeStruct(x.shape[::-1], BF16) for x in (a, b)),
+        in_specs=[vmem()] * 3,
+        out_specs=(vmem(),) * 2,
+        cost_estimate=cost(1),
+        compiler_params=pltpu.CompilerParams(vmem_limit_bytes=LIMIT),
+        name="turn",
+    )(after, a, b)
 
 
 def nt_dot(a, b):
@@ -111,6 +132,7 @@
             pl.BlockSpec((1, 8, TILE), lambda i: (at, 0, 0)),
         ),
         input_output_aliases={4 + i: i for i in range(len(so_far))},
+        cost_estimate=cost(1),
         compiler_params=pltpu.CompilerParams(vmem_limit_bytes=LIMIT),
         name="project",
     )(mine, other, w_key, w_value_t, *so_far)
@@ -138,9 +160,9 @@
 
     def gather(n, found):
         list_ref[found] = n
-        used = index_ref[start + n] >= 0
+        used = index_ref[0, start + n] >= 0
         for t in range(1, nodes // TILE):
-            used = used | (index_ref[start + t * tiles + n] >= 0)
+            used = used | (index_ref[0, start + t * tiles + n] >= 0)
         return found + jnp.where(used, 1, 0)
 
     found = lax.fori_loop(0, tiles, gather, 0)
@@ -152,7 +174,7 @@
         n = jnp.where(live, list_ref[i], 0)
         list_ref[i] = n
         for t in range(nodes // TILE):
-            e = index_ref[start + t * tiles + n]
+            e = index_ref[0, start + t * tiles + n]
             at = jnp.maximum(e, 0)
             words = jnp.where(n // 2 % 2 == 0, mine_ref[at], other_ref[at])
             words = jnp.where(live & (e >= 0), words, 0)
@@ -277,13 +299,22 @@
             VMEM((HEADS, 1, nodes), F32),
             SMEM((room + 1,), jnp.int32),
         ],
+        cost_estimate=cost(4),
         compiler_params=pltpu.CompilerParams(vmem_limit_bytes=LIMIT),
         name="attend",
     )(table, mine, other, feats, w_query_t, keys, values_t, norms)
 
 
 def finish_kernel(*refs):
-    parts, (w_ref, out_ref) = refs[:-2], refs[-2:]
+    count = (len(refs) - 4) // 2
+    own, far, (w_ref, out_ref) = refs[0], refs[1 : count + 1], refs[count + 1 : count + 3]
+    near, sems = refs[count + 3 : -1], refs[-1]
+    copies = [pltpu.make_async_copy(a, b, sems.at[i]) for i, (a, b) in enumerate(zip(far, near))]
+    for copy in copies:
+        copy.start()
+    for copy in copies:
+        copy.wait()
+    parts = [own] + list(near)
     width = w_ref.shape[0]
     size = width // HEADS
     tops, dens = [], []
@@ -316,11 +347,14 @@
 
 def finish(parts, w_out):
     nodes = parts[0].shape[1]
+    others = len(parts) - 1
     return pl.pallas_call(
         finish_kernel,
         out_shape=jax.ShapeDtypeStruct((nodes, w_out.shape[1]), BF16),
-        in_specs=[vmem()] * (len(parts) + 1),
+        in_specs=[vmem()] + [pl.BlockSpec(memory_space=pl.ANY)] * others + [vmem()],
         out_specs=vmem(),
+        scratch_shapes=[VMEM(parts[0].shape, BF16)] * others + [pltpu.SemaphoreType.DMA((others,))],
+        compiler_params=pltpu.CompilerParams(vmem_limit_bytes=LIMIT),
         name="finish",
     )(*parts, w_out)
 
@@ -329,30 +363,32 @@
     nrow, ncol = lax.axis_size("row"), lax.axis_size("col")
     nodes, _ = features.shape
     per = nodes // TILE
-    row, col = lax.axis_index("row"), lax.axis_index("col")
     chips = ncol // 2
     tiles = 2 * nrow * per
-    entries = pairs.shape[2]
 
     asking = [features] + [None] * (chips - 1)
     near = [features] + [None] * (nrow - 1)
-    far = list(range(chips // 2, chips)) + list(range(1, chips // 2))
-    for s in range(1, nrow):
+    half = chips // 2
+    asking[half] = exchange(features, "col", 2 * half)
+    for s in range(nrow - 1, 0, -1):
         near[s] = exchange(features, "row", s)
-    for s in far:
+    for s in range(1, half):
         asking[s] = exchange(features, "col", 2 * s)
+        asking[s + half] = exchange(asking[half], "col", 2 * s)
     mine = jnp.swapaxes(masks[0, 0], 1, 2)
     other = exchange(mine, "col", 1)
-    listed = jnp.concatenate([pairs.reshape(-1), counts.reshape(-1)])
-    theirs = exchange(listed, "col", 1)
-    table = index(listed, theirs, row, col, chips * per * tiles, tiles, entries)
-
-    w_value_t, w_query_t = w_value.T, w_query.T
+    listed = jnp.swapaxes(pairs[0, 0], 0, 1)
+    other_listed = exchange(listed, "col", 1)
+    other_counts = exchange(counts, "col", 1)
+    table = index(listed, counts, other_listed, other_counts, chips * per * tiles, tiles)
+    w_query_t, w_value_t = turn(table, w_query, w_value)
+
     ready = ()
     for s in range(nrow):
         twin = exchange(near[s], "col", 1)
         ready = project(near[s], twin, w_key, w_value_t, ready, s, nrow)
 
+    far = list(range(half, chips)) + list(range(1, half))
     parts = [None] * chips
     for s in far + [0]:
         part = attend(table, mine, other, asking[s], w_query_t, *ready, s, 2)

time: 136 us -> 122 us (0.90)
  Pallas kernels: 107 us -> 99.2 us
  local copies, waits for them, and re-layouts: 6.82 us -> 1.18 us
    unnamed x29 -> x14, local copies, waits for them, and re-layouts: 6.69 us -> 1.18 us
    pallas_call x1 -> x2, Pallas kernels: 5.93 us -> 1.12 us  [the longest x1 0.8 us: index(): pl.pallas_call(functools.partial(index_kernel, tiles=tiles), out_shape=ja...]
    ppermute x15 -> x16, waiting for transfers between devices: 3.92 us -> 4.89 us  [exchange(): return lax.ppermute(x, axis, [(i, i ^ bits) for i in range(size)])]
    ppermute x15 -> x16, starting transfers between devices: 16.2 us -> 15.4 us  [exchange(): return lax.ppermute(x, axis, [(i, i ^ bits) for i in range(size)])]
  transfers between devices with their start and end apart: 15 -> 16, of which waited for: 2 -> 3; matrix products, arithmetic and copies ran while one was open for 3% -> 0% of each run, Pallas kernels for 77% -> 80%
where the time goes in v1:
time: 122 us
  Pallas kernels  99.2 us (81%)
  starting transfers between devices  15.4 us (13%)
  waiting for transfers between devices  4.89 us (4%)
    pallas_call x4, Pallas kernels, attend(): pl.pallas_call(functools.partial(attend_kernel, chunk=chunk, sinks=sinks)...  93.3 us
    ppermute x16, starting transfers between devices, exchange(): return lax.ppermute(x, axis, [(i, i ^ bits) for i in range(size)])  15.4 us
    ppermute x16, waiting for transfers between devices, exchange(): return lax.ppermute(x, axis, [(i, i ^ bits) for i in range(size)])  4.89 us
    pallas_call x4, Pallas kernels, project(): pl.pallas_call(project_kernel, grid=(1,), out_shape=(jax.ShapeDtypeStruct...  3.4 us
  transfers between devices with their start and end apart: 16, of which 3 were waited for; matrix products, arithmetic and copies ran while one was open for 0% of the time, Pallas kernels for 80%

profile of v1, /device:TPU:7, one launch (start us, length us, event | category | flops | bytes accessed | tf_op | source)
XLA Modules:
  0.0 121.6 jit_solution(1706310734514847891)
XLA Ops:
  0.0 0.3 collective-permute-start.7
  0.3 0.0 collective-permute-start.5
  0.3 2.4 %collective-permute-start.3 = (bf16[256,512]{1,0:T(8,128)(2,1)}, bf16[256,512]{1,0:T(8,128)(2,1)S(1)}, u32[]{:S(2)}, u32[]{:S(2)}) collective-permute-start(bf16[256,512]{1,0:T(8,128)(2,1)} %f_ref.1), channel_id=1, source_target_pairs={{0,24},{8,16},{16,8},{24,0},{1,25},{9,17},{17,9},{25,1},{2,26},{10... | collective-permute-start | bytes 786440 | tf_op jit(solution)/shard_map/ppermute | solution.py:33
  2.7 1.5 %collective-permute-start = (s32[2,128]{1,0:T(2,128)}, s32[2,128]{1,0:T(2,128)S(1)}, u32[]{:S(2)}, u32[]{:S(2)}) collective-permute-start(s32[2,128]{1,0:T(2,128)} %bitcast.11), channel_id=1, source_target_pairs={{0,1},{1,0},{2,3},{3,2},{4,5},{5,4},{6,7},{7,6},{8,9},{9,8},{10,11... | collective-permute-start | bytes 3080 | tf_op jit(solution)/shard_map/ppermute | solution.py:33
  4.2 0.0 collective-permute-start.1
  4.8 0.6 collective-permute-done.1.other_count_ref
  5.4 0.2 collective-permute-start.9
  5.6 0.0 collective-permute-done.other_ref
  5.6 2.3 %collective-permute-start.12 = (bf16[256,512]{1,0:T(8,128)(2,1)}, bf16[256,512]{1,0:T(8,128)(2,1)S(1)}, u32[]{:S(2)}, u32[]{:S(2)}) collective-permute-start(bf16[256,512]{1,0:T(8,128)(2,1)} %f_ref.1), channel_id=1, source_target_pairs={{0,4},{1,5},{2,6},{3,7},{4,0},{5,1},{6,2},{7,3},{8,12},{9,13},{10,... | collective-permute-start | bytes 786440 | tf_op jit(solution)/shard_map/ppermute | solution.py:33
  7.9 0.0 collective-permute-done.7.mine_ref
  7.9 2.1 %collective-permute-start.8 = (bf16[256,512]{1,0:T(8,128)(2,1)S(1)}, bf16[256,512]{1,0:T(8,128)(2,1)S(1)}, u32[]{:S(2)}, u32[]{:S(2)}) collective-permute-start(bf16[256,512]{1,0:T(8,128)(2,1)S(1)} %collective-permute-done.7.mine_ref), channel_id=1, source_target_pairs={{0,1},{1,0},{2,3},{3,2},{4,5},{5,4},{6,7},{7,6},{8,9},{9,8},{10,11... | collective-permute-start | bytes 786440 | tf_op jit(solution)/shard_map/ppermute | solution.py:33
  10.1 0.0 collective-permute-done.5.mine_ref
  10.1 4.7 %collective-permute-start.6 = (bf16[256,512]{1,0:T(8,128)(2,1)S(1)}, bf16[256,512]{1,0:T(8,128)(2,1)S(1)}, u32[]{:S(2)}, u32[]{:S(2)}) collective-permute-start(bf16[256,512]{1,0:T(8,128)(2,1)S(1)} %collective-permute-done.5.mine_ref), channel_id=1, source_target_pairs={{0,1},{1,0},{2,3},{3,2},{4,5},{5,4},{6,7},{7,6},{8,9},{9,8},{10,11... | collective-permute-start | bytes 786440 | tf_op jit(solution)/shard_map/ppermute | solution.py:33
  14.8 0.7 copy-done.6
  15.5 0.8 index.1.after_ref.index_ref
  16.3 0.0 copy-start.4
  16.3 0.0 copy-start
  16.3 0.0 copy-start.5
  16.3 0.0 collective-permute-done.3.mine_ref
  16.3 0.1 collective-permute-start.4
  16.4 0.3 turn.1
  16.8 0.0 collective-permute-done.9.other_ref
  16.8 0.5 copy-done.4
  17.2 0.1 collective-permute-start.2
  17.3 2.6 %collective-permute-done.12.f_ref = bf16[256,512]{1,0:T(8,128)(2,1)S(1)} collective-permute-done((bf16[256,512]{1,0:T(8,128)(2,1)}, bf16[256,512]{1,0:T(8,128)(2,1)S(1)}, u32[]{:S(2)}, u32[]{:S(2)}) %collective-permute-start.12) | collective-permute-done | bytes 262176 | tf_op jit(solution)/shard_map/ppermute | solution.py:33
  19.9 1.2 collective-permute-start.14
  21.1 0.8 project.4
  22.0 0.0 collective-permute-done.8.other_ref
  22.0 0.3 collective-permute-start.10
  22.3 0.8 project.5
  23.2 0.0 collective-permute-done.6.other_ref
  23.2 0.9 project.6
  24.0 0.0 collective-permute-done.4.other_ref
  24.0 0.9 project.7
  24.9 0.0 collective-permute-done.2.other_ref
  24.9 1.7 %collective-permute-done.14.f_ref = bf16[256,512]{1,0:T(8,128)(2,1)S(1)} collective-permute-done((bf16[256,512]{1,0:T(8,128)(2,1)S(1)}, bf16[256,512]{1,0:T(8,128)(2,1)S(1)}, u32[]{:S(2)}, u32[]{:S(2)}) %collective-permute-start.14) | collective-permute-done | bytes 262176 | tf_op jit(solution)/shard_map/ppermute | solution.py:33
  26.6 24.4 %attend.7 = bf16[560,256]{1,0:T(8,128)(2,1)S(1)} custom-call(s32[1,128]{1,0:T(1,128)S(1)} %index.1.after_ref.index_ref, s32[128,4,128]{2,1,0:T(4,128)S(1)} %bitcast.7, s32[128,4,128]{2,1,0:T(4,128)S(1)} %collective-permute-done.2.other_ref, bf16[256,512]{1,0:T(8,128)(2,1)S(1)} %collective-permute-done.14.f_ref, ...), custom_call_target="tpu_custom_call" | custom-call | flops 3600000000 | tf_op jit(solution)/shard_map/attend/pallas_call | solution.py:290
  51.0 0.1 collective-permute-start.15
  51.1 22.9 %attend.6 = bf16[560,256]{1,0:T(8,128)(2,1)S(1)} custom-call(s32[1,128]{1,0:T(1,128)S(1)} %index.1.after_ref.index_ref, s32[128,4,128]{2,1,0:T(4,128)S(1)} %bitcast.8, s32[128,4,128]{2,1,0:T(4,128)S(1)} %collective-permute-done.2.other_ref, bf16[256,512]{1,0:T(8,128)(2,1)S(1)} %collective-permute-done.12.f_ref, ...), custom_call_target="tpu_custom_call" | custom-call | flops 3600000000 | tf_op jit(solution)/shard_map/attend/pallas_call | solution.py:290
  74.1 0.1 collective-permute-start.13
  74.2 0.0 collective-permute-done.10.f_ref
  74.2 24.4 %attend.5 = bf16[560,256]{1,0:T(8,128)(2,1)S(1)} custom-call(s32[1,128]{1,0:T(1,128)S(1)} %index.1.after_ref.index_ref, s32[128,4,128]{2,1,0:T(4,128)S(1)} %bitcast.9, s32[128,4,128]{2,1,0:T(4,128)S(1)} %collective-permute-done.2.other_ref, bf16[256,512]{1,0:T(8,128)(2,1)S(1)} %collective-permute-done.10.f_ref, ...), custom_call_target="tpu_custom_call" | custom-call | flops 3600000000 | tf_op jit(solution)/shard_map/attend/pallas_call | solution.py:290
  98.6 0.0 copy-start.1
  98.6 0.1 collective-permute-start.11
  98.7 21.4 %attend.4.refs_0_ = bf16[560,256]{1,0:T(8,128)(2,1)S(1)} custom-call(s32[1,128]{1,0:T(1,128)S(1)} %index.1.after_ref.index_ref, s32[128,4,128]{2,1,0:T(4,128)S(1)} %bitcast.10, s32[128,4,128]{2,1,0:T(4,128)S(1)} %collective-permute-done.2.other_ref, bf16[256,512]{1,0:T(8,128)(2,1)S(1)} %copy-done.5, bf16[512,512]{1,0:T(8,128)(2,1)S(1)} %get-tuple-element.19.wqt_ref, ...), custom_call_target="tpu_custom_call" | custom-call | flops 3600000000 | tf_op jit(solution)/shard_map/attend/pallas_call | solution.py:290
  120.1 0.0 collective-permute-done.15.refs_3_
  120.2 0.0 collective-permute-done.13.refs_2_
  120.2 1.4 %finish.1 = bf16[256,512]{1,0:T(8,128)(2,1)} custom-call(bf16[560,256]{1,0:T(8,128)(2,1)S(1)} %attend.4.refs_0_, bf16[560,256]{1,0:T(8,128)(2,1)S(1)} %collective-permute-done.11.refs_1_, bf16[560,256]{1,0:T(8,128)(2,1)S(1)} %collective-permute-done.13.refs_2_, bf16[560,256]{1,0:T(8,128)(2,1)S(1)} %collective-permute-done.15.refs_3_, ...), custom_call_target="tpu_custom_call" | custom-call | tf_op jit(solution)/shard_map/finish/pallas_call | solution.py:351
  (9 shorter events, 0.0 us)
Async XLA Ops:
  0.0 7.9 %collective-permute-start.7 = (bf16[256,512]{1,0:T(8,128)(2,1)}, bf16[256,512]{1,0:T(8,128)(2,1)S(1)}, u32[]{:S(2)}, u32[]{:S(2)}) collective-permute-start(bf16[256,512]{1,0:T(8,128)(2,1)} %f_ref.1), channel_id=1, source_target_pairs={{0,8},{8,0},{16,24},{24,16},{1,9},{9,1},{17,25},{25,17},{2,10},{10... | collective-permute-start | bytes 786440 | tf_op jit(solution)/shard_map/ppermute | solution.py:33
  0.3 9.8 %collective-permute-start.5 = (bf16[256,512]{1,0:T(8,128)(2,1)}, bf16[256,512]{1,0:T(8,128)(2,1)S(1)}, u32[]{:S(2)}, u32[]{:S(2)}) collective-permute-start(bf16[256,512]{1,0:T(8,128)(2,1)} %f_ref.1), channel_id=1, source_target_pairs={{0,16},{8,24},{16,0},{24,8},{1,17},{9,25},{17,1},{25,9},{2,18},{10... | collective-permute-start | bytes 786440 | tf_op jit(solution)/shard_map/ppermute | solution.py:33
  0.3 16.1 %collective-permute-start.3 = (bf16[256,512]{1,0:T(8,128)(2,1)}, bf16[256,512]{1,0:T(8,128)(2,1)S(1)}, u32[]{:S(2)}, u32[]{:S(2)}) collective-permute-start(bf16[256,512]{1,0:T(8,128)(2,1)} %f_ref.1), channel_id=1, source_target_pairs={{0,24},{8,16},{16,8},{24,0},{1,25},{9,17},{17,9},{25,1},{2,26},{10... | collective-permute-start | bytes 786440 | tf_op jit(solution)/shard_map/ppermute | solution.py:33
  2.7 3.0 %collective-permute-start = (s32[2,128]{1,0:T(2,128)}, s32[2,128]{1,0:T(2,128)S(1)}, u32[]{:S(2)}, u32[]{:S(2)}) collective-permute-start(s32[2,128]{1,0:T(2,128)} %bitcast.11), channel_id=1, source_target_pairs={{0,1},{1,0},{2,3},{3,2},{4,5},{5,4},{6,7},{7,6},{8,9},{9,8},{10,11... | collective-permute-start | bytes 3080 | tf_op jit(solution)/shard_map/ppermute | solution.py:33
  4.2 1.3 %collective-permute-start.1 = (s32[1,1]{1,0:T(1,128)}, s32[1,1]{1,0:T(1,128)}, u32[]{:S(2)}, u32[]{:S(2)}) collective-permute-start(s32[1,1]{1,0:T(1,128)} %param.14), channel_id=1, source_target_pairs={{0,1},{1,0},{2,3},{3,2},{4,5},{5,4},{6,7},{7,6},{8,9},{9,8},{10,11... | collective-permute-start | bytes 20 | tf_op jit(solution)/shard_map/ppermute | solution.py:33
  4.8 11.6 %copy-start.2 = (bf16[512,512]{1,0:T(8,128)(2,1)S(1)}, bf16[512,512]{1,0:T(8,128)(2,1)}, u32[]{:S(2)}) copy-start(bf16[512,512]{1,0:T(8,128)(2,1)} %a_ref.1) | copy-start | bytes 1572868
  4.8 11.6 %copy-start.3 = (bf16[512,512]{1,0:T(8,128)(2,1)S(1)}, bf16[512,512]{1,0:T(8,128)(2,1)}, u32[]{:S(2)}) copy-start(bf16[512,512]{1,0:T(8,128)(2,1)} %b_ref.1) | copy-start | bytes 1572868
  5.4 11.3 %collective-permute-start.9 = (bf16[256,512]{1,0:T(8,128)(2,1)}, bf16[256,512]{1,0:T(8,128)(2,1)S(1)}, u32[]{:S(2)}, u32[]{:S(2)}) collective-permute-start(bf16[256,512]{1,0:T(8,128)(2,1)} %f_ref.1), channel_id=1, source_target_pairs={{0,1},{1,0},{2,3},{3,2},{4,5},{5,4},{6,7},{7,6},{8,9},{9,8},{10,11... | collective-permute-start | bytes 786440 | tf_op jit(solution)/shard_map/ppermute | solution.py:33
  5.6 14.3 %collective-permute-start.12 = (bf16[256,512]{1,0:T(8,128)(2,1)}, bf16[256,512]{1,0:T(8,128)(2,1)S(1)}, u32[]{:S(2)}, u32[]{:S(2)}) collective-permute-start(bf16[256,512]{1,0:T(8,128)(2,1)} %f_ref.1), channel_id=1, source_target_pairs={{0,4},{1,5},{2,6},{3,7},{4,0},{5,1},{6,2},{7,3},{8,12},{9,13},{10,... | collective-permute-start | bytes 786440 | tf_op jit(solution)/shard_map/ppermute | solution.py:33
  7.9 14.0 %collective-permute-start.8 = (bf16[256,512]{1,0:T(8,128)(2,1)S(1)}, bf16[256,512]{1,0:T(8,128)(2,1)S(1)}, u32[]{:S(2)}, u32[]{:S(2)}) collective-permute-start(bf16[256,512]{1,0:T(8,128)(2,1)S(1)} %collective-permute-done.7.mine_ref), channel_id=1, source_target_pairs={{0,1},{1,0},{2,3},{3,2},{4,5},{5,4},{6,7},{7,6},{8,9},{9,8},{10,11... | collective-permute-start | bytes 786440 | tf_op jit(solution)/shard_map/ppermute | solution.py:33
  10.1 13.1 %collective-permute-start.6 = (bf16[256,512]{1,0:T(8,128)(2,1)S(1)}, bf16[256,512]{1,0:T(8,128)(2,1)S(1)}, u32[]{:S(2)}, u32[]{:S(2)}) collective-permute-start(bf16[256,512]{1,0:T(8,128)(2,1)S(1)} %collective-permute-done.5.mine_ref), channel_id=1, source_target_pairs={{0,1},{1,0},{2,3},{3,2},{4,5},{5,4},{6,7},{7,6},{8,9},{9,8},{10,11... | collective-permute-start | bytes 786440 | tf_op jit(solution)/shard_map/ppermute | solution.py:33
  14.8 0.7 copy-start.6
  16.3 1.0 copy-start.4
  16.3 4.8 %copy-start = (bf16[512,512]{1,0:T(8,128)(2,1)S(1)}, bf16[512,512]{1,0:T(8,128)(2,1)}, u32[]{:S(2)}) copy-start(bf16[512,512]{1,0:T(8,128)(2,1)} %wk_ref.7) | copy-start | bytes 1572868
  16.3 4.8 %copy-start.5 = (bf16[256,512]{1,0:T(8,128)(2,1)S(1)}, bf16[256,512]{1,0:T(8,128)(2,1)}, u32[]{:S(2)}) copy-start(bf16[256,512]{1,0:T(8,128)(2,1)} %f_ref.1) | copy-start | bytes 786436
  16.3 7.7 %collective-permute-start.4 = (bf16[256,512]{1,0:T(8,128)(2,1)S(1)}, bf16[256,512]{1,0:T(8,128)(2,1)S(1)}, u32[]{:S(2)}, u32[]{:S(2)}) collective-permute-start(bf16[256,512]{1,0:T(8,128)(2,1)S(1)} %collective-permute-done.3.mine_ref), channel_id=1, source_target_pairs={{0,1},{1,0},{2,3},{3,2},{4,5},{5,4},{6,7},{7,6},{8,9},{9,8},{10,11... | collective-permute-start | bytes 786440 | tf_op jit(solution)/shard_map/ppermute | solution.py:33
  17.2 7.7 %collective-permute-start.2 = (s32[128,4,128]{2,1,0:T(4,128)S(1)}, s32[128,4,128]{2,1,0:T(4,128)S(1)}, u32[]{:S(2)}, u32[]{:S(2)}) collective-permute-start(s32[128,4,128]{2,1,0:T(4,128)S(1)} %bitcast.6), channel_id=1, source_target_pairs={{0,1},{1,0},{2,3},{3,2},{4,5},{5,4},{6,7},{7,6},{8,9},{9,8},{10,11... | collective-permute-start | bytes 786440 | tf_op jit(solution)/shard_map/ppermute | solution.py:33
  19.9 6.7 %collective-permute-start.14 = (bf16[256,512]{1,0:T(8,128)(2,1)S(1)}, bf16[256,512]{1,0:T(8,128)(2,1)S(1)}, u32[]{:S(2)}, u32[]{:S(2)}) collective-permute-start(bf16[256,512]{1,0:T(8,128)(2,1)S(1)} %collective-permute-done.12.f_ref), channel_id=1, source_target_pairs={{0,2},{1,3},{2,0},{3,1},{4,6},{5,7},{6,4},{7,5},{8,10},{9,11},{10,... | collective-permute-start | bytes 786440 | tf_op jit(solution)/shard_map/ppermute | solution.py:33
  22.0 52.2 %collective-permute-start.10 = (bf16[256,512]{1,0:T(8,128)(2,1)S(1)}, bf16[256,512]{1,0:T(8,128)(2,1)S(1)}, u32[]{:S(2)}, u32[]{:S(2)}) collective-permute-start(bf16[256,512]{1,0:T(8,128)(2,1)S(1)} %copy-done.5), channel_id=1, source_target_pairs={{0,2},{1,3},{2,0},{3,1},{4,6},{5,7},{6,4},{7,5},{8,10},{9,11},{10,... | collective-permute-start | bytes 786440 | tf_op jit(solution)/shard_map/ppermute | solution.py:33
  51.0 69.1 %collective-permute-start.15 = (bf16[560,256]{1,0:T(8,128)(2,1)S(1)}, bf16[560,256]{1,0:T(8,128)(2,1)S(1)}, u32[]{:S(2)}, u32[]{:S(2)}) collective-permute-start(bf16[560,256]{1,0:T(8,128)(2,1)S(1)} %attend.7), channel_id=1, source_target_pairs={{0,6},{1,7},{2,4},{3,5},{4,2},{5,3},{6,0},{7,1},{8,14},{9,15},{10,... | collective-permute-start | bytes 860168 | tf_op jit(solution)/shard_map/ppermute | solution.py:33
  74.1 46.1 %collective-permute-start.13 = (bf16[560,256]{1,0:T(8,128)(2,1)S(1)}, bf16[560,256]{1,0:T(8,128)(2,1)S(1)}, u32[]{:S(2)}, u32[]{:S(2)}) collective-permute-start(bf16[560,256]{1,0:T(8,128)(2,1)S(1)} %attend.6), channel_id=1, source_target_pairs={{0,4},{1,5},{2,6},{3,7},{4,0},{5,1},{6,2},{7,3},{8,12},{9,13},{10,... | collective-permute-start | bytes 860168 | tf_op jit(solution)/shard_map/ppermute | solution.py:33
  98.6 21.6 %copy-start.1 = (bf16[512,512]{1,0:T(8,128)(2,1)S(1)}, bf16[512,512]{1,0:T(8,128)(2,1)}, u32[]{:S(2)}) copy-start(bf16[512,512]{1,0:T(8,128)(2,1)} %refs_4_.1) | copy-start | bytes 1572868
  98.6 21.5 %collective-permute-start.11 = (bf16[560,256]{1,0:T(8,128)(2,1)S(1)}, bf16[560,256]{1,0:T(8,128)(2,1)S(1)}, u32[]{:S(2)}, u32[]{:S(2)}) collective-permute-start(bf16[560,256]{1,0:T(8,128)(2,1)S(1)} %attend.5), channel_id=1, source_target_pairs={{0,2},{1,3},{2,0},{3,1},{4,6},{5,7},{6,4},{7,5},{8,10},{9,11},{10,... | collective-permute-start | bytes 860168 | tf_op jit(solution)/shard_map/ppermute | solution.py:33
